TPU v7x, 32 devices: a 4x4x1 block of a 4x4x8 slice. The times are simulated.
32 devices in a mesh: rep: 2 (over z, core), dp: 16 (over x, y).
Axes of the slice: x: 4, y: 4, z: 1, core: 2. Of those that a mesh axis runs over, the one named last changes fastest.
The devices are a block of a 4x4x8 slice.
Arguments:
- x: bfloat16 [32, 2048, 512], P(('rep', 'dp')), parts along dimension 0
- dy: bfloat16 [32, 2048, 512], P(('rep', 'dp')), parts along dimension 0
- w_gate: bfloat16 [2, 512, 2048], replicated
- w_up: bfloat16 [2, 512, 2048], replicated
- w_down: bfloat16 [2, 2048, 512], replicated
- m_w_gate: float32 [2, 512, 2048], replicated
- m_w_up: float32 [2, 512, 2048], replicated
- m_w_down: float32 [2, 2048, 512], replicated
- v_w_gate: float32 [2, 512, 2048], replicated
- v_w_up: float32 [2, 512, 2048], replicated
- v_w_down: float32 [2, 2048, 512], replicated
Outputs:
- output 1: bfloat16 [4, 512, 2048], P('rep'), parts along dimension 0
- output 2: bfloat16 [4, 512, 2048], P('rep'), parts along dimension 0
- output 3: bfloat16 [4, 2048, 512], P('rep'), parts along dimension 0
- output 4: float32 [4, 512, 2048], P('rep'), parts along dimension 0
- output 5: float32 [4, 512, 2048], P('rep'), parts along dimension 0
- output 6: float32 [4, 2048, 512], P('rep'), parts along dimension 0
- output 7: float32 [4, 512, 2048], P('rep'), parts along dimension 0
- output 8: float32 [4, 512, 2048], P('rep'), parts along dimension 0
- output 9: float32 [4, 2048, 512], P('rep'), parts along dimension 0
There are 2 independent parts. A program takes and returns all parts, laid end to end along the dimension named above; an argument that names none is the same for every part.
All inputs are finite; a program needn't handle non-finite values.
Results may differ from a plain program's by a relative error of at most 0.02.
Values are sent between devices in bfloat16 or wider.
A program may use at most 768 MiB of HBM per device.

v0:
```python
import jax
import jax.numpy as jnp
from jax import lax
from jax.sharding import PartitionSpec as P

NAMES = ("w_gate", "w_up", "w_down")


def matmul(a, w):
    return jnp.dot(a, w, preferred_element_type=jnp.float32).astype(jnp.bfloat16)


def normed(h):
    wide = h.astype(jnp.float32)
    scale = lax.rsqrt(jnp.mean(wide**2, -1, keepdims=True) + 1e-6)
    return (wide * scale).astype(jnp.bfloat16)


def layer(h, w):
    a = normed(h)
    gate = jnp.dot(a, w["w_gate"], preferred_element_type=jnp.float32)
    up = jnp.dot(a, w["w_up"], preferred_element_type=jnp.float32)
    return h + matmul((jax.nn.silu(gate) * up).astype(jnp.bfloat16), w["w_down"])


def adamw(w, m, v, g):
    m = 0.9 * m + 0.1 * g
    v = 0.95 * v + 0.05 * g * g
    step = m * lax.rsqrt(v + 1e-8) + 0.1 * w
    return (w - 0.02 * step).astype(jnp.bfloat16), m, v


def solution(mesh):
    def step(x, dy, *arrays):
        weights, m, v = (arrays[i : i + 3] for i in (0, 3, 6))
        layers = weights[0].shape[0]
        h, kept = x[0], []
        for number in range(layers):
            kept.append(h)
            h = layer(h, {name: w[number] for name, w in zip(NAMES, weights, strict=True)})
        by_h, summed = dy[0], [None] * layers
        for number in reversed(range(layers)):
            _, back = jax.vjp(lambda w, h: layer(h, w), {name: w[number] for name, w in zip(NAMES, weights, strict=True)}, kept[number])
            by_w, by_h = back(by_h)
            summed[number] = [lax.psum(by_w[name], "dp") for name in NAMES]
        gradients = [jnp.stack([summed[number][i] for number in range(layers)]).astype(jnp.float32) for i in range(3)]
        new = [adamw(w.astype(jnp.float32), m, v, g) for w, m, v, g in zip(weights, m, v, gradients, strict=True)]
        return tuple(one[which] for which in range(3) for one in new)

    return jax.shard_map(
        step,
        mesh=mesh,
        in_specs=(P(("rep", "dp"), None, None),) * 2 + (P(None, None, None),) * 9,
        out_specs=(P("rep", None, None),) * 9,
        check_vma=False,
    )
```

profile of v0, /device:TPU:96, one launch (start us, length us, event | category | flops | bytes accessed | tf_op | source)
XLA Modules:
  0.0 419.0 jit_solution(16411273446845654864)
XLA Ops:
  7.2 0.1 all-reduce.3.cloned.1.call-start
  7.3 2.9 copy.20
  10.2 0.0 copy-start
  10.2 0.5 fusion.30
  10.7 4.2 copy.21
  14.9 10.3 %convolution_convert_fusion.1 = bf16[2048,2048]{1,0:T(8,128)(2,1)} fusion(bf16[1,2048,512]{2,1,0:T(8,128)(2,1)} %param.12, bf16[2,2048,512]{2,1,0:T(8,128)(2,1)} %param.15), kind=kOutput, calls=%fused_computation.52 | convolution fusion | flops 4299161600 | bytes 12582912 | tf_op jit(solution)/shard_map/transpose(jvp())/dot_general | solution.py:10
  25.2 0.0 copy-done.3
  25.2 0.0 copy-done.10
  25.2 8.2 %fusion.70 = f32[2048,2048]{1,0:T(8,128)} fusion(bf16[2,512,2048]{2,1,0:T(8,128)(2,1)S(1)} %copy-done.3, bf16[1,2048,512]{2,1,0:T(8,128)(2,1)S(1)} %copy-done.10, f32[2048]{0:T(1024)S(1)} %add_rsqrt_fusion), kind=kOutput, calls=%fused_computation.103 | convolution fusion | flops 4298113024 | bytes 20979712 | tf_op jit(solution)/shard_map/dot_general | solution.py:21
  33.4 0.0 copy-done.16
  33.4 17.7 %multiply_convert_fusion.1 = (bf16[2048,2048]{1,0:T(8,128)(2,1)}, f32[2048,2048]{1,0:T(8,128)}) fusion(f32[2048,2048]{1,0:T(8,128)} %fusion.70, bf16[2,512,2048]{2,1,0:T(8,128)(2,1)} %param.14, bf16[1,2048,512]{2,1,0:T(8,128)(2,1)S(1)} %copy-done.10, f32[2048]{0:T(1024)S(1)} %add_rsqrt_fusion), kind=kOutput, calls=%fused_computation.17 | convolution fusion | flops 4323278848 | bytes 46145536 | tf_op jit(solution)/shard_map/dot_general | solution.py:22
  51.1 0.0 copy-done
  51.1 0.0 copy-start.6
  51.2 9.1 %fusion.34 = (f32[2048]{0:T(1024)S(1)}, bf16[2048,512]{0,1:T(8,128)(2,1)S(1)}) fusion(bf16[2048,2048]{1,0:T(8,128)(2,1)} %get-tuple-element.24, bf16[2,2048,512]{2,1,0:T(8,128)(2,1)} %param.15, bf16[1,2048,512]{1,2,0:T(8,128)(2,1)S(1)} %copy.20), kind=kOutput, calls=%fused_computation.64 | convolution fusion | flops 4300208128 | bytes 14688256 | tf_op jit(solution)/shard_map/dot_general | solution.py:10
  60.2 0.0 copy-start.12
  60.2 0.0 copy-start.14
  60.3 1.3 copy-done.12
  61.6 0.0 copy-done.14
  61.6 0.0 copy-done.6
  61.6 8.3 %fusion.59 = f32[2048,2048]{1,0:T(8,128)} fusion(bf16[2,512,2048]{2,1,0:T(8,128)(2,1)S(1)} %copy-done.6, bf16[2048,512]{0,1:T(8,128)(2,1)S(1)} %get-tuple-element.27, f32[2048]{0:T(1024)S(1)} %fusion.89), kind=kOutput, calls=%fused_computation.92 | convolution fusion | flops 4298113024 | bytes 20979712 | tf_op jit(solution)/shard_map/jvp()/dot_general | solution.py:22
  69.8 22.9 %fusion.2 = (bf16[2048,2048]{1,0:T(8,128)(2,1)}, f32[2048,2048]{1,0:T(8,128)}) fusion(f32[2048,2048]{1,0:T(8,128)} %fusion.59, bf16[2048,2048]{1,0:T(8,128)(2,1)} %convolution_convert_fusion.1, bf16[2,512,2048]{2,1,0:T(8,128)(2,1)} %param.13, bf16[2048,512]{0,1:T(8,128)(2,1)} %copy-done.12, f32[2048]{0:T(1024)S(1)} %fusion.89), kind=kOutput, calls=%fused_computation.8 | convolution fusion | flops 4348444672 | bytes 54534144 | tf_op jit(solution)/shard_map/jvp()/dot_general | solution.py:21
  92.8 0.0 copy-done.11
  92.8 14.5 %fusion.49 = bf16[1,2048,512]{2,1,0:T(8,128)(2,1)} fusion(f32[2048,2048]{1,0:T(8,128)} %fusion.59, bf16[1,2048,512]{2,1,0:T(8,128)(2,1)S(1)} %copy-done.11, f32[2048,2048]{1,0:T(8,128)} %get-tuple-element.29), kind=kOutput, calls=%fused_computation.84 | convolution fusion | flops 4321181696 | bytes 37748736 | tf_op jit(solution)/shard_map/transpose(jvp())/dot_general | solution.py:10
  107.2 0.0 copy-done.13
  107.2 12.4 %fusion.48 = bf16[1,512,2048]{2,1,0:T(8,128)(2,1)} fusion(bf16[2048,2048]{1,0:T(8,128)(2,1)} %convolution_convert_fusion.1, bf16[2048,512]{0,1:T(8,128)(2,1)S(1)} %copy-done.13, f32[2048]{0:T(1024)S(1)} %fusion.89, f32[2048,2048]{1,0:T(8,128)} %get-tuple-element.29), kind=kOutput, calls=%fused_computation.83 | convolution fusion | flops 4324327424 | bytes 29368320 | tf_op jit(solution)/shard_map/transpose(jvp())/dot_general | solution.py:22
  119.6 0.0 copy-done.7
  119.6 11.4 %fusion.41 = bf16[2048,512]{0,1:T(8,128)(2,1)S(1)} fusion(bf16[2048,2048]{1,0:T(8,128)(2,1)} %convolution_convert_fusion.1, bf16[2,512,2048]{2,1,0:T(8,128)(2,1)S(1)} %copy-done.7, f32[2048,2048]{1,0:T(8,128)} %get-tuple-element.29), kind=kOutput, calls=%fused_computation.75 | convolution fusion | flops 4321181696 | bytes 29360128 | tf_op jit(solution)/shard_map/transpose(jvp())/dot_general | solution.py:22
  131.0 0.0 copy-start.4
  131.0 9.3 %fusion.46 = bf16[1,512,2048]{2,1,0:T(8,128)(2,1)} fusion(bf16[2048,2048]{1,0:T(8,128)(2,1)} %get-tuple-element.28, bf16[2048,512]{0,1:T(8,128)(2,1)S(1)} %copy-done.13, f32[2048]{0:T(1024)S(1)} %fusion.89), kind=kOutput, calls=%fused_computation.81 | convolution fusion | flops 4298113024 | bytes 12591104 | tf_op jit(solution)/shard_map/transpose(jvp())/dot_general | solution.py:21
  140.3 0.0 copy-done.4
  140.3 9.0 %fusion.36 = (f32[2048]{0:T(1024)S(1)}, bf16[2048,512]{0,1:T(8,128)(2,1)S(1)}) fusion(bf16[2048,512]{0,1:T(8,128)(2,1)S(1)} %copy-done.13, bf16[2048,512]{0,1:T(8,128)(2,1)S(1)} %fusion.41, bf16[2048,2048]{1,0:T(8,128)(2,1)} %get-tuple-element.28, bf16[2,512,2048]{2,1,0:T(8,128)(2,1)S(1)} %copy-done.4), kind=kOutput, calls=%fused_computation.66 | convolution fusion | flops 4300208128 | bytes 16785408 | tf_op jit(solution)/shard_map/transpose(jvp())/dot_general | solution.py:21
  149.3 0.0 copy-done.15
  149.3 0.0 copy-done.2
  149.3 1.4 fusion.56
  150.7 0.0 copy-start.9
  150.7 9.7 %fusion.45 = bf16[1,2048,512]{2,1,0:T(8,128)(2,1)} fusion(bf16[2048,2048]{1,0:T(8,128)(2,1)} %get-tuple-element.24, bf16[2048,512]{0,1:T(8,128)(2,1)S(1)} %fusion.56), kind=kOutput, calls=%fused_computation.80 | convolution fusion | flops 4296015872 | bytes 12582912 | tf_op jit(solution)/shard_map/transpose(jvp())/dot_general | solution.py:10
  160.4 0.0 copy-done.9
  160.4 5.1 %convolution_convert_fusion = bf16[2048,2048]{1,0:T(8,128)(2,1)S(1)} fusion(bf16[2048,512]{0,1:T(8,128)(2,1)S(1)} %fusion.56, bf16[2,2048,512]{2,1,0:T(8,128)(2,1)S(1)} %copy-done.9), kind=kOutput, calls=%fused_computation.51 | convolution fusion | flops 4299161600 | bytes 12582912 | tf_op jit(solution)/shard_map/transpose(jvp())/dot_general | solution.py:10
  165.5 0.0 copy-done.1
  165.6 0.0 copy-done.17
  165.6 0.0 copy-start.18
  165.6 13.5 %fusion.47 = bf16[1,512,2048]{2,1,0:T(8,128)(2,1)} fusion(bf16[2048,2048]{1,0:T(8,128)(2,1)S(1)} %convolution_convert_fusion, f32[2048,2048]{1,0:T(8,128)} %fusion.70, bf16[1,2048,512]{1,2,0:T(8,128)(2,1)S(1)} %copy-done.1, f32[2048]{0:T(1024)S(1)} %copy-done.17), kind=kOutput, calls=%fused_computation.82 | convolution fusion | flops 4324327424 | bytes 29368320 | tf_op jit(solution)/shard_map/transpose(jvp())/dot_general | solution.py:22
  179.1 17.6 %fusion.50 = bf16[1,512,2048]{2,1,0:T(8,128)(2,1)} fusion(f32[2048,2048]{1,0:T(8,128)} %fusion.70, f32[2048,2048]{1,0:T(8,128)} %get-tuple-element.25, bf16[2048,2048]{1,0:T(8,128)(2,1)} %copy-done.18, bf16[1,2048,512]{1,2,0:T(8,128)(2,1)S(1)} %copy-done.1, f32[2048]{0:T(1024)S(1)} %copy-done.17), kind=kOutput, calls=%fused_computation.85 | convolution fusion | flops 4345298944 | bytes 46145536 | tf_op jit(solution)/shard_map/transpose(jvp())/dot_general | solution.py:21
  196.7 0.1 all-reduce.3.cloned.1.call-update
  196.7 170.5 %all-reduce.3.cloned.1.call-done = (bf16[1,512,2048]{2,1,0:T(8,128)(2,1)}, bf16[1,512,2048]{2,1,0:T(8,128)(2,1)}, bf16[1,512,2048]{2,1,0:T(8,128)(2,1)}, bf16[1,...) async-done(((bf16[1,512,2048]{2,1,0:T(8,128)(2,1)}, bf16[1,512,2048]{2,1,0:T(8,128)(2,1)}, bf16[1,512,2048]{2,1,0:T(8,128)(2,1)}, ...) | async-done | bytes 12582928 | tf_op jit(solution)/shard_map/psum | solution.py:45
  367.2 16.7 %fusion.23 = (bf16[2,2048,512]{2,1,0:T(8,128)(2,1)}, f32[2,2048,512]{2,1,0:T(8,128)}, f32[2,2048,512]{2,1,0:T(8,128)}) fusion(bf16[2,2048,512]{2,1,0:T(8,128)(2,1)} %param.15, bf16[1,2048,512]{2,1,0:T(8,128)(2,1)} %get-tuple-element.13, bf16[1,2048,512]{2,1,0:T(8,128)(2,1)} %get-tuple-element.14, f32[2,2048,512]{2,1,0:T(8,128)} %param.21, ...), kind=kLoop, calls=%fused_computation.44 | loop fusion | flops 39845888 | bytes 46137344 | tf_op jit(solution)/shard_map/convert_element_type | solution.py:30
  383.9 0.0 copy-done.8
  383.9 27.7 %fusion.15 = (bf16[2,512,2048]{2,1,0:T(8,128)(2,1)}, f32[2,512,2048]{2,1,0:T(8,128)}, f32[2,512,2048]{2,1,0:T(8,128)}, bf16[2,512,2048]{2,1,0:T(8,128)(2,1)}, f3...) fusion(bf16[2,512,2048]{2,1,0:T(8,128)(2,1)S(1)} %copy-done.5, bf16[1,512,2048]{2,1,0:T(8,128)(2,1)} %get-tuple-element.9, ...), kind=kLoop, calls=%fused_computation.36 | loop fusion | flops 79691776 | bytes 92274688 | tf_op jit(solution)/shard_map/convert_element_type | solution.py:30
  (17 shorter events, 0.1 us)
Async XLA Ops:
  7.2 360.0 %all-reduce.3.cloned.1.call-start = ((), (), s32[]{:S(2)}) async-start(), calls=%async_computation | async-start | bytes 25165824 | tf_op jit(solution)/shard_map/psum | solution.py:45
  10.2 40.9 %copy-start = (bf16[1,2048,512]{1,2,0:T(8,128)(2,1)}, bf16[1,2048,512]{1,2,0:T(8,128)(2,1)S(1)}, u32[]{:S(2)}) copy-start(bf16[1,2048,512]{1,2,0:T(8,128)(2,1)S(1)} %copy.20) | copy-start | bytes 6291460
  10.7 22.7 %copy-start.16 = (f32[2048]{0:T(1024)}, f32[2048]{0:T(1024)S(1)}, u32[]{:S(2)}) copy-start(f32[2048]{0:T(1024)S(1)} %add_rsqrt_fusion) | copy-start | bytes 24580
  14.8 10.3 %copy-start.3 = (bf16[2,512,2048]{2,1,0:T(8,128)(2,1)S(1)}, bf16[2,512,2048]{2,1,0:T(8,128)(2,1)}, u32[]{:S(2)}) copy-start(bf16[2,512,2048]{2,1,0:T(8,128)(2,1)} %param.13) | copy-start | bytes 12582916
  14.8 10.3 %copy-start.10 = (bf16[1,2048,512]{2,1,0:T(8,128)(2,1)S(1)}, bf16[1,2048,512]{2,1,0:T(8,128)(2,1)}, u32[]{:S(2)}) copy-start(bf16[1,2048,512]{2,1,0:T(8,128)(2,1)} %param.11) | copy-start | bytes 6291460
  51.1 10.4 %copy-start.6 = (bf16[2,512,2048]{2,1,0:T(8,128)(2,1)S(1)}, bf16[2,512,2048]{2,1,0:T(8,128)(2,1)}, u32[]{:S(2)}) copy-start(bf16[2,512,2048]{2,1,0:T(8,128)(2,1)} %param.14) | copy-start | bytes 12582916
  60.2 1.3 copy-start.12
  60.2 1.3 copy-start.14
  69.8 22.9 %copy-start.11 = (bf16[1,2048,512]{2,1,0:T(8,128)(2,1)S(1)}, bf16[1,2048,512]{2,1,0:T(8,128)(2,1)}, u32[]{:S(2)}) copy-start(bf16[1,2048,512]{2,1,0:T(8,128)(2,1)} %param.12) | copy-start | bytes 6291460
  92.8 14.5 %copy-start.13 = (bf16[2048,512]{0,1:T(8,128)(2,1)S(1)}, bf16[2048,512]{0,1:T(8,128)(2,1)}, u32[]{:S(2)}) copy-start(bf16[2048,512]{0,1:T(8,128)(2,1)} %copy-done.12) | copy-start | bytes 6291460
  107.2 12.4 %copy-start.7 = (bf16[2,512,2048]{2,1,0:T(8,128)(2,1)S(1)}, bf16[2,512,2048]{2,1,0:T(8,128)(2,1)}, u32[]{:S(2)}) copy-start(bf16[2,512,2048]{2,1,0:T(8,128)(2,1)} %param.14) | copy-start | bytes 12582916
  131.0 9.3 %copy-start.4 = (bf16[2,512,2048]{2,1,0:T(8,128)(2,1)S(1)}, bf16[2,512,2048]{2,1,0:T(8,128)(2,1)}, u32[]{:S(2)}) copy-start(bf16[2,512,2048]{2,1,0:T(8,128)(2,1)} %param.13) | copy-start | bytes 12582916
  140.3 9.0 %copy-start.15 = (f32[2048]{0:T(1024)S(1)}, f32[2048]{0:T(1024)}, u32[]{:S(2)}) copy-start(f32[2048]{0:T(1024)} %copy-done.14) | copy-start | bytes 24580
  140.3 9.1 %copy-start.2 = (bf16[1,2048,512]{1,2,0:T(8,128)(2,1)S(1)}, bf16[1,2048,512]{1,2,0:T(8,128)(2,1)}, u32[]{:S(2)}) copy-start(bf16[1,2048,512]{1,2,0:T(8,128)(2,1)} %copy.21) | copy-start | bytes 6291460
  150.7 9.7 %copy-start.9 = (bf16[2,2048,512]{2,1,0:T(8,128)(2,1)S(1)}, bf16[2,2048,512]{2,1,0:T(8,128)(2,1)}, u32[]{:S(2)}) copy-start(bf16[2,2048,512]{2,1,0:T(8,128)(2,1)} %param.15) | copy-start | bytes 12582916
  160.4 5.1 %copy-start.1 = (bf16[1,2048,512]{1,2,0:T(8,128)(2,1)S(1)}, bf16[1,2048,512]{1,2,0:T(8,128)(2,1)}, u32[]{:S(2)}) copy-start(bf16[1,2048,512]{1,2,0:T(8,128)(2,1)} %copy-done) | copy-start | bytes 6291460
  160.4 5.1 %copy-start.17 = (f32[2048]{0:T(1024)S(1)}, f32[2048]{0:T(1024)}, u32[]{:S(2)}) copy-start(f32[2048]{0:T(1024)} %copy-done.16) | copy-start | bytes 24580
  165.6 13.5 %copy-start.18 = (bf16[2048,2048]{1,0:T(8,128)(2,1)}, bf16[2048,2048]{1,0:T(8,128)(2,1)S(1)}, u32[]{:S(2)}) copy-start(bf16[2048,2048]{1,0:T(8,128)(2,1)S(1)} %convolution_convert_fusion) | copy-start | bytes 25165828
  367.2 16.7 %copy-start.5 = (bf16[2,512,2048]{2,1,0:T(8,128)(2,1)S(1)}, bf16[2,512,2048]{2,1,0:T(8,128)(2,1)}, u32[]{:S(2)}) copy-start(bf16[2,512,2048]{2,1,0:T(8,128)(2,1)} %param.13) | copy-start | bytes 12582916
  367.2 16.7 %copy-start.8 = (bf16[2,512,2048]{2,1,0:T(8,128)(2,1)S(1)}, bf16[2,512,2048]{2,1,0:T(8,128)(2,1)}, u32[]{:S(2)}) copy-start(bf16[2,512,2048]{2,1,0:T(8,128)(2,1)} %param.14) | copy-start | bytes 12582916
Sparse Core Ops, SparseCore 0:
  196.9 170.3 all-reduce.2
where the time goes:
time: 427 us; the launch traced here: 419 us
  matrix products  179 us (42%)
  waiting for transfers between devices  171 us (40%)
  other arithmetic  46.2 us (11%)
  between operations  14.8 us (3%)
  local copies, waits for them, and re-layouts  8.49 us (2%)
    psum x1, waiting for transfers between devices, step(): summed[number] = [lax.psum(by_w[name], 'dp') for name in NAMES]  170 us
    dot_general x5, matrix products, layer(): gate = jnp.dot(a, w['w_gate'], preferred_element_type=jnp.float32)  67 us
    dot_general x5, matrix products, layer(): up = jnp.dot(a, w['w_up'], preferred_element_type=jnp.float32)  63.2 us
    dot_general x5, matrix products, matmul(): jnp.dot(a, w, preferred_element_type=jnp.float32).astype(jnp.bfloat16)  48.7 us
    convert_element_type x2, other arithmetic, adamw(): return ((w - 0.02 * step).astype(jnp.bfloat16), m, v)  44.4 us
  transfers between devices with their start and end apart: 1, of which 1 were waited for; matrix products, arithmetic and copies ran while one was open for 0% of the time, Pallas kernels for 0%

commit v1 on v0

v1 whole, which is shorter than its diff:
```python
import functools
import math

import jax
import jax.numpy as jnp
from jax import lax
from jax.experimental import pallas as pl
from jax.experimental.pallas import tpu as pltpu
from jax.sharding import PartitionSpec as P

F32 = jnp.float32
BF16 = jnp.bfloat16
BLOCK = 512
TILE = 256
ROUNDS = 4


def dot(a, b):
    return jnp.dot(a, b, preferred_element_type=F32)


def dot_nt(a, b):
    return lax.dot_general(a, b, (((1,), (1,)), ((), ())), preferred_element_type=F32)


def normed(wide):
    return wide * lax.rsqrt(jnp.mean(wide * wide, -1, keepdims=True) + 1e-6)


def train_kernel(n, x_hbm, dy_hbm, wg_hbm, wu_hbm, wd_hbm, out_hbm,
                 h, dy, a, at, dyt, prod, dg, du, dag, dau, wg, wu, wd,
                 mine, got_a, got_b, got_c, got_d, part, stage, whole,
                 in_sem, w_sem, rs_send, rs_recv, ag_send, ag_recv, out_sem):
    layers, d, ff = wg_hbm.shape
    tokens = x_hbm.shape[1]
    blocks = ff // BLOCK
    chunks = layers * blocks
    tiles = tokens // TILE
    side = math.isqrt(n)
    chunk_rows = mine.shape[1]
    half = chunk_rows // 2
    klass = half // side
    piece = klass // side
    cols = mine.shape[2]
    hc = cols // 2

    me = lax.axis_index("dp")
    cx, cy = me // side, me % side

    def near(c, by):
        return (c + by + side) % side

    ids = {
        "x": (near(cx, 1) * side + cy, near(cx, -1) * side + cy),
        "y": (cx * side + near(cy, 1), cx * side + near(cy, -1)),
    }
    sides = ((0, cx, cy, ids["x"], ids["y"]), (1, cy, cx, ids["y"], ids["x"]))

    def rows(base, size):
        return pl.ds(pl.multiple_of(base, 16), size)

    left, right = pl.ds(0, hc), pl.ds(hc, hc)
    lanes = (left, right)

    x_copy = pltpu.make_async_copy(x_hbm.at[0], h.at[0], in_sem.at[0])
    dy_copy = pltpu.make_async_copy(dy_hbm.at[0], dy, in_sem.at[1])

    def w_copies(l, j):
        span = pl.ds(j * BLOCK, BLOCK)
        return (
            pltpu.make_async_copy(wg_hbm.at[l, :, span], wg.at[l, j], w_sem.at[0, l, j]),
            pltpu.make_async_copy(wu_hbm.at[l, :, span], wu.at[l, j], w_sem.at[1, l, j]),
            pltpu.make_async_copy(wd_hbm.at[l, span, :], wd.at[l, j], w_sem.at[2, l, j]),
        )

    x_copy.start()
    for l in range(layers):
        for j in range(blocks):
            for copy in w_copies(l, j):
                copy.start()
    dy_copy.start()

    barrier = pltpu.get_barrier_semaphore()
    for other in (*ids["x"], *ids["y"]):
        pl.semaphore_signal(barrier, inc=1, device_id={"dp": other}, device_id_type=pl.DeviceIdType.MESH)
    pl.semaphore_wait(barrier, 4)

    def rs_copy(c, hf, rnd, way, src, dst, to):
        slot = c % 2
        return pltpu.make_async_remote_copy(
            src_ref=src, dst_ref=dst, send_sem=rs_send.at[slot, hf, rnd, way], recv_sem=rs_recv.at[slot, hf, rnd, way],
            device_id={"dp": to}, device_id_type=pl.DeviceIdType.MESH)

    def rs_round(c, rnd):
        slot = c % 2
        copies = []
        for hf, f, s, fid, sid in sides:
            base = hf * half
            for way, by in ((0, 1), (1, -1)):
                if rnd == 0:
                    src = mine.at[slot, rows(base + near(f, 2) * klass, klass), lanes[way]]
                    dst, to = got_a.at[slot, hf, way], fid[way]
                elif rnd == 1:
                    src = mine.at[slot, rows(base + near(f, by) * klass, klass), :]
                    dst, to = got_b.at[slot, hf, way], fid[way]
                elif rnd == 2:
                    src = stage.at[slot, hf, 2, :, lanes[way]]
                    dst, to = got_c.at[slot, hf, way], sid[way]
                else:
                    src = stage.at[slot, hf, way]
                    dst, to = got_d.at[slot, hf, way], sid[way]
                copies.append(rs_copy(c, hf, rnd, way, src, dst, to))
        return copies

    def rs_event(c, e):
        slot = c % 2
        if e > 0:
            for copy in rs_round(c, e - 1):
                copy.wait()
        for hf, f, s, fid, sid in sides:
            base = hf * half
            if e == 1:
                for way, by in ((0, 1), (1, -1)):
                    span = rows(base + near(f, by) * klass, klass)
                    total = mine[slot, span, lanes[way]].astype(F32) + got_a[slot, hf, way].astype(F32)
                    mine[slot, span, lanes[way]] = total.astype(BF16)
            elif e == 2:
                total = mine[slot, rows(base + f * klass, klass), :].astype(F32)
                part[slot, hf] = total + got_b[slot, hf, 0].astype(F32) + got_b[slot, hf, 1].astype(F32)
                stage[slot, hf, 2] = part[slot, hf, rows(near(s, 2) * piece, piece), :].astype(BF16)
            elif e == 3:
                for way, by in ((0, 1), (1, -1)):
                    span = rows(near(s, by) * piece, piece)
                    total = part[slot, hf, span, lanes[way]] + got_c[slot, hf, way].astype(F32)
                    stage[slot, hf, way, :, lanes[way]] = total.astype(BF16)
                    stage[slot, hf, way, :, lanes[1 - way]] = part[slot, hf, span, lanes[1 - way]].astype(BF16)
            elif e == 4:
                total = part[slot, hf, rows(s * piece, piece), :]
                total = total + got_d[slot, hf, 0].astype(F32) + got_d[slot, hf, 1].astype(F32)
                whole[c, rows(base + f * klass + s * piece, piece), :] = total.astype(BF16)
        if e < ROUNDS:
            for copy in rs_round(c, e):
                copy.start()

    def ag_round(c, rnd):
        copies = []
        for hf, f, s, fid, sid in sides:
            base = hf * half
            for way, by in ((0, 1), (1, -1)):
                if rnd == 0:
                    ref = whole.at[c, rows(base + f * klass + s * piece, piece), :]
                elif rnd == 1:
                    ref = whole.at[c, rows(base + f * klass + near(s, -by) * piece, piece), lanes[way]]
                elif rnd == 2:
                    ref = whole.at[c, rows(base + f * klass, klass), :]
                else:
                    ref = whole.at[c, rows(base + near(f, -by) * klass, klass), lanes[way]]
                to = sid[way] if rnd < 2 else fid[way]
                copies.append(pltpu.make_async_remote_copy(
                    src_ref=ref, dst_ref=ref, send_sem=ag_send.at[c, hf, rnd, way], recv_sem=ag_recv.at[c, hf, rnd, way],
                    device_id={"dp": to}, device_id_type=pl.DeviceIdType.MESH))
        return copies

    def out_copy(c):
        return pltpu.make_async_copy(whole.at[c], out_hbm.at[c], out_sem.at[c])

    def ag_event(c, e):
        if e > 0:
            for copy in ag_round(c, e - 1):
                copy.wait()
        if e < ROUNDS:
            for copy in ag_round(c, e):
                copy.start()
        else:
            out_copy(c).start()

    def guarded(low, high, c, event, e):
        pl.when((c >= low) & (c < high))(lambda: event(c, e))

    def first_ticks(c):
        guarded(0, chunks, c - 2, rs_event, 3)
        guarded(0, chunks, c - 1, rs_event, 1)

    def second_ticks(c):
        guarded(0, chunks, c - 2, rs_event, 4)
        guarded(0, chunks, c - 1, rs_event, 2)
        guarded(0, chunks, c, rs_event, 0)

    x_copy.wait()
    for l in range(layers - 1):
        for j in range(blocks):
            for copy in w_copies(l, j):
                copy.wait()

        def forward(t, _):
            span = rows(t * TILE, TILE)
            wide = h[l, span, :].astype(F32)
            av = normed(wide).astype(BF16)
            acc = None
            for j in range(blocks):
                gate, up = dot(av, wg[l, j]), dot(av, wu[l, j])
                p = (gate * jax.nn.sigmoid(gate) * up).astype(BF16)
                term = dot(p, wd[l, j])
                acc = term if acc is None else acc + term
            h[l + 1, span, :] = (wide + acc.astype(BF16).astype(F32)).astype(BF16)
            return 0

        lax.fori_loop(0, tiles, forward, 0)

    for j in range(blocks):
        for copy in w_copies(layers - 1, j):
            copy.wait()
    dy_copy.wait()

    for number, l in enumerate(reversed(range(layers))):
        need = l > 0

        def enter(t, _):
            span = rows(t * TILE, TILE)
            across = pl.ds(pl.multiple_of(t * TILE, 128), TILE)
            av = normed(h[l, span, :].astype(F32))
            a[span, :] = av.astype(BF16)
            at[:, across] = av.T.astype(BF16)
            dyt[:, across] = dy[span, :].astype(F32).T.astype(BF16)
            if need:
                dag[span, :] = jnp.zeros((TILE, d), F32)
                dau[span, :] = jnp.zeros((TILE, d), F32)
            return 0

        lax.fori_loop(0, tiles, enter, 0)

        def block(j, _):
            c = number * blocks + j
            slot = c % 2

            def tile(t, _):
                span = rows(t * TILE, TILE)
                av, dyv = a[span, :], dy[span, :]
                gate, up = dot(av, wg[l, j]), dot(av, wu[l, j])
                dp = dot_nt(dyv, wd[l, j]).astype(BF16).astype(F32)
                sig = jax.nn.sigmoid(gate)
                act = gate * sig
                prod[span, :] = (act * up).astype(BF16)
                dgv = (dp * up * (sig + act * (1.0 - sig))).astype(BF16)
                duv = (dp * act).astype(BF16)
                dg[span, :] = dgv
                du[span, :] = duv
                if need:
                    dag[span, :] += dot_nt(dgv, wg[l, j])
                    dau[span, :] += dot_nt(duv, wu[l, j])
                return 0

            cut = tiles * 3 // 4 if need else tiles
            lax.fori_loop(0, cut, tile, 0)
            first_ticks(c)
            if cut < tiles:
                lax.fori_loop(cut, tiles, tile, 0)

            def grads(q, _):
                span = rows(q * 256, 256)
                mine[slot, span, :] = dot(at[span, :], dg[...]).astype(BF16)
                mine[slot, rows(d + q * 256, 256), :] = dot(at[span, :], du[...]).astype(BF16)
                across = pl.ds(pl.multiple_of(q * 256, 128), 256)
                mine[slot, 2 * d : 2 * d + BLOCK, across] = dot(dyt[span, :], prod[...]).T.astype(BF16)
                return 0

            lax.fori_loop(0, d // 256, grads, 0)
            second_ticks(c)
            return 0

        lax.fori_loop(0, blocks, block, 0)

        if need:

            def leave(t, _):
                span = rows(t * TILE, TILE)
                da = (dag[span, :].astype(BF16).astype(F32) + dau[span, :].astype(BF16).astype(F32)).astype(BF16).astype(F32)
                wide = h[l, span, :].astype(F32)
                scale = lax.rsqrt(jnp.mean(wide * wide, -1, keepdims=True) + 1e-6)
                by_scale = jnp.sum(da * wide, -1, keepdims=True)
                by_wide = da * scale - wide * (by_scale * scale * scale * scale * (1.0 / d))
                dy[span, :] = (dy[span, :].astype(F32) + by_wide.astype(BF16).astype(F32)).astype(BF16)
                return 0

            lax.fori_loop(0, tiles, leave, 0)

    def drain(k, _):
        for e in (4, 3, 2, 1):
            guarded(0, chunks, k - e, ag_event, e)
        pl.when(k == 0)(lambda: first_ticks(chunks))
        pl.when(k == 1)(lambda: second_ticks(chunks))
        pl.when(k == 2)(lambda: first_ticks(chunks + 1))
        pl.when(k == 3)(lambda: second_ticks(chunks + 1))
        guarded(0, chunks, k, ag_event, 0)
        return 0

    lax.fori_loop(0, chunks + ROUNDS, drain, 0)
    for c in range(chunks):
        out_copy(c).wait()


def summed_gradients(n, x, dy, wg, wu, wd):
    layers, d, ff = wg.shape
    tokens = x.shape[1]
    blocks = ff // BLOCK
    chunks = layers * blocks
    side = math.isqrt(n)
    chunk_rows = 2 * d + BLOCK
    klass = chunk_rows // 2 // side
    piece = klass // side
    hbm = pl.BlockSpec(memory_space=pl.ANY)
    dma = pltpu.SemaphoreType.DMA
    return pl.pallas_call(
        functools.partial(train_kernel, n),
        out_shape=jax.ShapeDtypeStruct((chunks, chunk_rows, d), BF16),
        in_specs=[hbm] * 5,
        out_specs=hbm,
        scratch_shapes=[
            pltpu.VMEM((layers, tokens, d), BF16),
            pltpu.VMEM((tokens, d), BF16),
            pltpu.VMEM((tokens, d), BF16),
            pltpu.VMEM((d, tokens), BF16),
            pltpu.VMEM((d, tokens), BF16),
            pltpu.VMEM((tokens, BLOCK), BF16),
            pltpu.VMEM((tokens, BLOCK), BF16),
            pltpu.VMEM((tokens, BLOCK), BF16),
            pltpu.VMEM((tokens, d), F32),
            pltpu.VMEM((tokens, d), F32),
            pltpu.VMEM((layers, blocks, d, BLOCK), BF16),
            pltpu.VMEM((layers, blocks, d, BLOCK), BF16),
            pltpu.VMEM((layers, blocks, BLOCK, d), BF16),
            pltpu.VMEM((2, chunk_rows, d), BF16),
            pltpu.VMEM((2, 2, 2, klass, d // 2), BF16),
            pltpu.VMEM((2, 2, 2, klass, d), BF16),
            pltpu.VMEM((2, 2, 2, piece, d // 2), BF16),
            pltpu.VMEM((2, 2, 2, piece, d), BF16),
            pltpu.VMEM((2, 2, klass, d), F32),
            pltpu.VMEM((2, 2, 3, piece, d), BF16),
            pltpu.VMEM((chunks, chunk_rows, d), BF16),
            dma((2,)),
            dma((3, layers, blocks)),
            dma((2, 2, ROUNDS, 2)),
            dma((2, 2, ROUNDS, 2)),
            dma((chunks, 2, ROUNDS, 2)),
            dma((chunks, 2, ROUNDS, 2)),
            dma((chunks,)),
        ],
        compiler_params=pltpu.CompilerParams(collective_id=0, has_side_effects=True, vmem_limit_bytes=67043328),
        name="train",
    )(x, dy, wg, wu, wd)


def adamw_kernel(g, *refs):
    ins, outs = refs[:9], refs[9:]
    for i in range(3):
        w, m, v = (ins[i + 3 * k] for k in range(3))
        gv = g[0, i].astype(F32)
        mv = 0.9 * m[0] + 0.1 * gv
        vv = 0.95 * v[0] + 0.05 * gv * gv
        wv = w[0].astype(F32)
        step = mv * lax.rsqrt(vv + 1e-8) + 0.1 * wv
        outs[i][0] = (wv - 0.02 * step).astype(BF16)
        outs[i + 3][0] = mv
        outs[i + 6][0] = vv


def adamw(g, arrays):
    layers, d, ff = arrays[0].shape
    blocks = ff // BLOCK
    cut = 2
    size = d // cut
    g = g.reshape(layers * blocks, 3, d, BLOCK)
    wide = pl.BlockSpec((1, size, BLOCK), lambda c, r: (layers - 1 - c // blocks, r, c % blocks))
    tall = pl.BlockSpec((1, size, d), lambda c, r: (layers - 1 - c // blocks, (c % blocks) * cut + r, 0))
    specs = [wide, wide, tall] * 3
    return pl.pallas_call(
        adamw_kernel,
        grid=(layers * blocks, cut),
        out_shape=[jax.ShapeDtypeStruct(v.shape, v.dtype) for v in arrays],
        in_specs=[pl.BlockSpec((1, 3, size, BLOCK), lambda c, r: (c, 0, r, 0)), *specs],
        out_specs=specs,
        compiler_params=pltpu.CompilerParams(vmem_limit_bytes=60 * 2**20),
        name="adamw",
    )(g, *arrays)


def solution(mesh):
    n = mesh.shape["dp"]

    def step(x, dy, *arrays):
        g = summed_gradients(n, x, dy, *arrays[:3])
        return tuple(adamw(g, arrays))

    return jax.shard_map(
        step,
        mesh=mesh,
        in_specs=(P(("rep", "dp"), None, None),) * 2 + (P(None, None, None),) * 9,
        out_specs=(P("rep", None, None),) * 9,
        check_vma=False,
    )
```

time: 427 us -> 272 us (0.64); the launches traced: 419 us -> 272 us
  Pallas kernels: 0 us -> 271 us
  matrix products: 179 us -> 0 us
  waiting for transfers between devices: 171 us -> 0 us
  other arithmetic: 46.2 us -> 0 us
  between operations: 14.8 us -> 0.65 us
  local copies, waits for them, and re-layouts: 8.49 us -> 0 us
    pallas_call x0 -> x2, Pallas kernels: none -> 271 us  [the longest x1 223 us: summed_gradients(): pl.pallas_call(functools.partial(train_kernel, n), out_shape=jax.ShapeDty...]
    dot_general x15 -> x0, matrix products: 179 us -> none  [the longest x5 67 us: layer(): gate = jnp.dot(a, w['w_gate'], preferred_element_type=jnp.float32)]
    psum x1 -> x0, waiting for transfers between devices: 170 us -> none  [step(): summed[number] = [lax.psum(by_w[name], 'dp') for name in NAMES]]
    convert_element_type x2 -> x0, other arithmetic: 44.4 us -> none  [adamw(): return ((w - 0.02 * step).astype(jnp.bfloat16), m, v)]
    unnamed x40 -> x0, local copies, waits for them, and re-layouts: 8.49 us -> none
  transfers between devices with their start and end apart: 1 -> 0, of which waited for: 1 -> 0; matrix products, arithmetic and copies ran while one was open for 0% -> 0% of each run, Pallas kernels for 0% -> 0%
where the time goes in v1:
time: 272 us
  Pallas kernels  271 us (100%)
    pallas_call x1, Pallas kernels, summed_gradients(): pl.pallas_call(functools.partial(train_kernel, n), out_shape=jax.ShapeDty...  223 us
    pallas_call x1, Pallas kernels, adamw(): pl.pallas_call(adamw_kernel, grid=(layers * blocks, cut), out_shape=[jax....  48.3 us

profile of v1, /device:TPU:96, one launch (start us, length us, event | category | flops | bytes accessed | tf_op | source)
XLA Modules:
  0.0 271.8 jit_solution(6264819562665152857)
XLA Ops:
  0.6 222.8 %train.1 = bf16[8,1536,512]{2,1,0:T(8,128)(2,1)} custom-call(bf16[1,2048,512]{2,1,0:T(8,128)(2,1)} %x_hbm.1, bf16[1,2048,512]{2,1,0:T(8,128)(2,1)} %dy_hbm.1, bf16[2,512,2048]{2,1,0:T(8,128)(2,1)} %refs_0_.1, bf16[2,512,2048]{2,1,0:T(8,128)(2,1)} %refs_1_.1, bf16[2,2048,512]{2,1,0:T(8,128)(2,1)} %refs_2_.1), custom_call_target="tpu_custom_call" | custom-call | tf_op jit(solution)/shard_map/train/pallas_call | solution.py:313
  223.5 48.3 %adamw.1 = (bf16[2,512,2048]{2,1,0:T(8,128)(2,1)}, bf16[2,512,2048]{2,1,0:T(8,128)(2,1)}, bf16[2,2048,512]{2,1,0:T(8,128)(2,1)}, f32[2,512,2048]{2,1,0:T(8,128)}...) custom-call(bf16[8,3,512,512]{3,2,1,0:T(8,128)(2,1)} %bitcast.1, ...), custom_call_target="tpu_custom_call" | custom-call | tf_op jit(solution)/shard_map/adamw/pallas_call | solution.py:376

commit v2 on v1

--- a/solution.py
+++ b/solution.py
@@ -11,8 +11,10 @@
 F32 = jnp.float32
 BF16 = jnp.bfloat16
 BLOCK = 512
-TILE = 256
+TILE = 512
 ROUNDS = 4
+SCATTER_AT = (0, 1, 3, 4, 5)
+GATHER_AT = (5, 6, 9, 12, 15)
 
 
 def dot(a, b):
@@ -23,12 +25,16 @@
     return lax.dot_general(a, b, (((1,), (1,)), ((), ())), preferred_element_type=F32)
 
 
+def sigmoid(x):
+    return 0.5 * jnp.tanh(0.5 * x) + 0.5
+
+
 def normed(wide):
     return wide * lax.rsqrt(jnp.mean(wide * wide, -1, keepdims=True) + 1e-6)
 
 
 def train_kernel(n, x_hbm, dy_hbm, wg_hbm, wu_hbm, wd_hbm, out_hbm,
-                 h, dy, a, at, dyt, prod, dg, du, dag, dau, wg, wu, wd,
+                 h, dy, a, at, dyt, prod, dg, du, dag, dau, weights,
                  mine, got_a, got_b, got_c, got_d, part, stage, whole,
                  in_sem, w_sem, rs_send, rs_recv, ag_send, ag_recv, out_sem):
     layers, d, ff = wg_hbm.shape
@@ -62,16 +68,23 @@
     left, right = pl.ds(0, hc), pl.ds(hc, hc)
     lanes = (left, right)
 
+    w_rows = (pl.ds(0, d), pl.ds(d, d), pl.ds(2 * d, BLOCK))
+
+    def w_place(l, j):
+        return (whole, chunks - blocks + j) if l == layers - 1 else (weights, l * blocks + j)
+
+    def w_read(l, j, k):
+        ref, i = w_place(l, j)
+        return ref[i, w_rows[k], :]
+
     x_copy = pltpu.make_async_copy(x_hbm.at[0], h.at[0], in_sem.at[0])
     dy_copy = pltpu.make_async_copy(dy_hbm.at[0], dy, in_sem.at[1])
 
     def w_copies(l, j):
         span = pl.ds(j * BLOCK, BLOCK)
-        return (
-            pltpu.make_async_copy(wg_hbm.at[l, :, span], wg.at[l, j], w_sem.at[0, l, j]),
-            pltpu.make_async_copy(wu_hbm.at[l, :, span], wu.at[l, j], w_sem.at[1, l, j]),
-            pltpu.make_async_copy(wd_hbm.at[l, span, :], wd.at[l, j], w_sem.at[2, l, j]),
-        )
+        ref, i = w_place(l, j)
+        sources = (wg_hbm.at[l, :, span], wu_hbm.at[l, :, span], wd_hbm.at[l, span, :])
+        return [pltpu.make_async_copy(src, ref.at[i, w_rows[k], :], w_sem.at[k, l, j]) for k, src in enumerate(sources)]
 
     x_copy.start()
     for l in range(layers):
@@ -174,17 +187,12 @@
         else:
             out_copy(c).start()
 
-    def guarded(low, high, c, event, e):
-        pl.when((c >= low) & (c < high))(lambda: event(c, e))
-
-    def first_ticks(c):
-        guarded(0, chunks, c - 2, rs_event, 3)
-        guarded(0, chunks, c - 1, rs_event, 1)
-
-    def second_ticks(c):
-        guarded(0, chunks, c - 2, rs_event, 4)
-        guarded(0, chunks, c - 1, rs_event, 2)
-        guarded(0, chunks, c, rs_event, 0)
+    def tick(b, odd):
+        due = [(at, 0, e) for e, at in enumerate(SCATTER_AT)] + [(at, 1, e) for e, at in enumerate(GATHER_AT)]
+        for at, gather, e in sorted(due, key=lambda one: (-((one[0] + 1) // 2), one[1], one[2])):
+            if (at + 1) % 2 == odd:
+                c = b - (at + 1) // 2
+                pl.when((c >= 0) & (c < chunks))(functools.partial(ag_event if gather else rs_event, c, e))
 
     x_copy.wait()
     for l in range(layers - 1):
@@ -198,9 +206,9 @@
             av = normed(wide).astype(BF16)
             acc = None
             for j in range(blocks):
-                gate, up = dot(av, wg[l, j]), dot(av, wu[l, j])
-                p = (gate * jax.nn.sigmoid(gate) * up).astype(BF16)
-                term = dot(p, wd[l, j])
+                gate, up = dot(av, w_read(l, j, 0)), dot(av, w_read(l, j, 1))
+                p = (gate * sigmoid(gate) * up).astype(BF16)
+                term = dot(p, w_read(l, j, 2))
                 acc = term if acc is None else acc + term
             h[l + 1, span, :] = (wide + acc.astype(BF16).astype(F32)).astype(BF16)
             return 0
@@ -236,9 +244,9 @@
             def tile(t, _):
                 span = rows(t * TILE, TILE)
                 av, dyv = a[span, :], dy[span, :]
-                gate, up = dot(av, wg[l, j]), dot(av, wu[l, j])
-                dp = dot_nt(dyv, wd[l, j]).astype(BF16).astype(F32)
-                sig = jax.nn.sigmoid(gate)
+                gate, up = dot(av, w_read(l, j, 0)), dot(av, w_read(l, j, 1))
+                dp = dot_nt(dyv, w_read(l, j, 2)).astype(BF16).astype(F32)
+                sig = sigmoid(gate)
                 act = gate * sig
                 prod[span, :] = (act * up).astype(BF16)
                 dgv = (dp * up * (sig + act * (1.0 - sig))).astype(BF16)
@@ -246,13 +254,13 @@
                 dg[span, :] = dgv
                 du[span, :] = duv
                 if need:
-                    dag[span, :] += dot_nt(dgv, wg[l, j])
-                    dau[span, :] += dot_nt(duv, wu[l, j])
+                    dag[span, :] += dot_nt(dgv, w_read(l, j, 0))
+                    dau[span, :] += dot_nt(duv, w_read(l, j, 1))
                 return 0
 
             cut = tiles * 3 // 4 if need else tiles
             lax.fori_loop(0, cut, tile, 0)
-            first_ticks(c)
+            tick(c, 0)
             if cut < tiles:
                 lax.fori_loop(cut, tiles, tile, 0)
 
@@ -265,7 +273,7 @@
                 return 0
 
             lax.fori_loop(0, d // 256, grads, 0)
-            second_ticks(c)
+            tick(c, 1)
             return 0
 
         lax.fori_loop(0, blocks, block, 0)
@@ -284,17 +292,12 @@
 
             lax.fori_loop(0, tiles, leave, 0)
 
-    def drain(k, _):
-        for e in (4, 3, 2, 1):
-            guarded(0, chunks, k - e, ag_event, e)
-        pl.when(k == 0)(lambda: first_ticks(chunks))
-        pl.when(k == 1)(lambda: second_ticks(chunks))
-        pl.when(k == 2)(lambda: first_ticks(chunks + 1))
-        pl.when(k == 3)(lambda: second_ticks(chunks + 1))
-        guarded(0, chunks, k, ag_event, 0)
+    def drain(b, _):
+        tick(b, 0)
+        tick(b, 1)
         return 0
 
-    lax.fori_loop(0, chunks + ROUNDS, drain, 0)
+    lax.fori_loop(chunks, chunks + (GATHER_AT[-1] + 1) // 2, drain, 0)
     for c in range(chunks):
         out_copy(c).wait()
 
@@ -326,9 +329,7 @@
             pltpu.VMEM((tokens, BLOCK), BF16),
             pltpu.VMEM((tokens, d), F32),
             pltpu.VMEM((tokens, d), F32),
-            pltpu.VMEM((layers, blocks, d, BLOCK), BF16),
-            pltpu.VMEM((layers, blocks, d, BLOCK), BF16),
-            pltpu.VMEM((layers, blocks, BLOCK, d), BF16),
+            pltpu.VMEM(((layers - 1) * blocks, chunk_rows, d), BF16),
             pltpu.VMEM((2, chunk_rows, d), BF16),
             pltpu.VMEM((2, 2, 2, klass, d // 2), BF16),
             pltpu.VMEM((2, 2, 2, klass, d), BF16),
@@ -367,7 +368,7 @@
 def adamw(g, arrays):
     layers, d, ff = arrays[0].shape
     blocks = ff // BLOCK
-    cut = 2
+    cut = 1
     size = d // cut
     g = g.reshape(layers * blocks, 3, d, BLOCK)
     wide = pl.BlockSpec((1, size, BLOCK), lambda c, r: (layers - 1 - c // blocks, r, c % blocks))

time: 272 us -> 233 us (0.86)
  Pallas kernels: 271 us -> 232 us
    pallas_call x1, Pallas kernels: 223 us -> 188 us  [summed_gradients(): pl.pallas_call(functools.partial(train_kernel, n), out_shape=jax.ShapeDty...]
    pallas_call x1, Pallas kernels: 48.3 us -> 43.6 us  [adamw(): pl.pallas_call(adamw_kernel, grid=(layers * blocks, cut), out_shape=[jax....]
where the time goes in v2:
time: 233 us
  Pallas kernels  232 us (100%)
    pallas_call x1, Pallas kernels, summed_gradients(): pl.pallas_call(functools.partial(train_kernel, n), out_shape=jax.ShapeDty...  188 us
    pallas_call x1, Pallas kernels, adamw(): pl.pallas_call(adamw_kernel, grid=(layers * blocks, cut), out_shape=[jax....  43.6 us

profile of v2, /device:TPU:96, one launch (start us, length us, event | category | flops | bytes accessed | tf_op | source)
XLA Modules:
  0.0 232.6 jit_solution(4609772082359658110)
XLA Ops:
  0.6 188.2 %train.1 = bf16[8,1536,512]{2,1,0:T(8,128)(2,1)} custom-call(bf16[1,2048,512]{2,1,0:T(8,128)(2,1)} %x_hbm.1, bf16[1,2048,512]{2,1,0:T(8,128)(2,1)} %dy_hbm.1, bf16[2,512,2048]{2,1,0:T(8,128)(2,1)} %refs_0_.1, bf16[2,512,2048]{2,1,0:T(8,128)(2,1)} %refs_1_.1, bf16[2,2048,512]{2,1,0:T(8,128)(2,1)} %refs_2_.1), custom_call_target="tpu_custom_call" | custom-call | tf_op jit(solution)/shard_map/train/pallas_call | solution.py:316
  188.9 43.6 %adamw.1 = (bf16[2,512,2048]{2,1,0:T(8,128)(2,1)}, bf16[2,512,2048]{2,1,0:T(8,128)(2,1)}, bf16[2,2048,512]{2,1,0:T(8,128)(2,1)}, f32[2,512,2048]{2,1,0:T(8,128)}...) custom-call(bf16[8,3,512,512]{3,2,1,0:T(8,128)(2,1)} %bitcast.1, ...), custom_call_target="tpu_custom_call" | custom-call | tf_op jit(solution)/shard_map/adamw/pallas_call | solution.py:377

commit v3 on v2

--- a/solution.py
+++ b/solution.py
@@ -13,8 +13,9 @@
 BLOCK = 512
 TILE = 512
 ROUNDS = 4
-SCATTER_AT = (0, 1, 3, 4, 5)
-GATHER_AT = (5, 6, 9, 12, 15)
+AHEAD = 16
+SCATTER_AT = (0, 1, 3, 5, 7)
+GATHER_AT = (7, 8, 10, 13, 17)
 
 
 def dot(a, b):
@@ -34,7 +35,7 @@
 
 
 def train_kernel(n, x_hbm, dy_hbm, wg_hbm, wu_hbm, wd_hbm, out_hbm,
-                 h, dy, a, at, dyt, prod, dg, du, dag, dau, weights,
+                 h, dy, a, at, dyt, prod, dg, du, weights,
                  mine, got_a, got_b, got_c, got_d, part, stage, whole,
                  in_sem, w_sem, rs_send, rs_recv, ag_send, ag_recv, out_sem):
     layers, d, ff = wg_hbm.shape
@@ -42,6 +43,7 @@
     blocks = ff // BLOCK
     chunks = layers * blocks
     tiles = tokens // TILE
+    period = blocks + tiles // 2
     side = math.isqrt(n)
     chunk_rows = mine.shape[1]
     half = chunk_rows // 2
@@ -191,12 +193,14 @@
         due = [(at, 0, e) for e, at in enumerate(SCATTER_AT)] + [(at, 1, e) for e, at in enumerate(GATHER_AT)]
         for at, gather, e in sorted(due, key=lambda one: (-((one[0] + 1) // 2), one[1], one[2])):
             if (at + 1) % 2 == odd:
-                c = b - (at + 1) // 2
-                pl.when((c >= 0) & (c < chunks))(functools.partial(ag_event if gather else rs_event, c, e))
+                back = b - (at + 1) // 2 + period * AHEAD
+                number, j = lax.div(back, period) - AHEAD, lax.rem(back, period)
+                event = functools.partial(ag_event if gather else rs_event, number * blocks + j, e)
+                pl.when((number >= 0) & (number < layers) & (j < blocks))(event)
 
     x_copy.wait()
     for l in range(layers - 1):
-        for j in range(blocks):
+        def arrived(l, j):
             for copy in w_copies(l, j):
                 copy.wait()
 
@@ -206,6 +210,7 @@
             av = normed(wide).astype(BF16)
             acc = None
             for j in range(blocks):
+                pl.when(t == 0)(functools.partial(arrived, l, j))
                 gate, up = dot(av, w_read(l, j, 0)), dot(av, w_read(l, j, 1))
                 p = (gate * sigmoid(gate) * up).astype(BF16)
                 term = dot(p, w_read(l, j, 2))
@@ -220,22 +225,37 @@
             copy.wait()
     dy_copy.wait()
 
+    def enter(l, t):
+        span = rows(t * TILE, TILE)
+        across = pl.ds(pl.multiple_of(t * TILE, 128), TILE)
+        av = normed(h[l, span, :].astype(F32)).astype(BF16)
+        a[span, :] = av
+        at[:, across] = av.T
+        dyt[:, across] = dy[span, :].T
+
+    def leave(l, t):
+        span = rows(t * TILE, TILE)
+
+        def back(grads, k):
+            total = None
+            for j in range(blocks):
+                term = dot_nt(grads[j, span, :], w_read(l, j, k))
+                total = term if total is None else total + term
+            return total.astype(BF16).astype(F32)
+
+        da = (back(dg, 0) + back(du, 1)).astype(BF16).astype(F32)
+        wide = h[l, span, :].astype(F32)
+        scale = lax.rsqrt(jnp.mean(wide * wide, -1, keepdims=True) + 1e-6)
+        by_scale = jnp.sum(da * wide, -1, keepdims=True)
+        by_wide = da * scale - wide * (by_scale * scale * scale * scale * (1.0 / d))
+        dy[span, :] = (dy[span, :].astype(F32) + by_wide.astype(BF16).astype(F32)).astype(BF16)
+
+    def first(t, _):
+        enter(layers - 1, t)
+        return 0
+
+    lax.fori_loop(0, tiles, first, 0)
     for number, l in enumerate(reversed(range(layers))):
-        need = l > 0
-
-        def enter(t, _):
-            span = rows(t * TILE, TILE)
-            across = pl.ds(pl.multiple_of(t * TILE, 128), TILE)
-            av = normed(h[l, span, :].astype(F32))
-            a[span, :] = av.astype(BF16)
-            at[:, across] = av.T.astype(BF16)
-            dyt[:, across] = dy[span, :].astype(F32).T.astype(BF16)
-            if need:
-                dag[span, :] = jnp.zeros((TILE, d), F32)
-                dau[span, :] = jnp.zeros((TILE, d), F32)
-            return 0
-
-        lax.fori_loop(0, tiles, enter, 0)
 
         def block(j, _):
             c = number * blocks + j
@@ -251,53 +271,37 @@
                 prod[span, :] = (act * up).astype(BF16)
                 dgv = (dp * up * (sig + act * (1.0 - sig))).astype(BF16)
                 duv = (dp * act).astype(BF16)
-                dg[span, :] = dgv
-                du[span, :] = duv
-                if need:
-                    dag[span, :] += dot_nt(dgv, w_read(l, j, 0))
-                    dau[span, :] += dot_nt(duv, w_read(l, j, 1))
+                dg[j, span, :] = dgv
+                du[j, span, :] = duv
                 return 0
 
-            cut = tiles * 3 // 4 if need else tiles
-            lax.fori_loop(0, cut, tile, 0)
-            tick(c, 0)
-            if cut < tiles:
-                lax.fori_loop(cut, tiles, tile, 0)
-
-            def grads(q, _):
-                span = rows(q * 256, 256)
-                mine[slot, span, :] = dot(at[span, :], dg[...]).astype(BF16)
-                mine[slot, rows(d + q * 256, 256), :] = dot(at[span, :], du[...]).astype(BF16)
-                across = pl.ds(pl.multiple_of(q * 256, 128), 256)
-                mine[slot, 2 * d : 2 * d + BLOCK, across] = dot(dyt[span, :], prod[...]).T.astype(BF16)
-                return 0
-
-            lax.fori_loop(0, d // 256, grads, 0)
-            tick(c, 1)
+            lax.fori_loop(0, tiles, tile, 0)
+            tick(number * period + j, 0)
+            mine[slot, 0:d, :] = dot(at[...], dg[j]).astype(BF16)
+            mine[slot, d : 2 * d, :] = dot(at[...], du[j]).astype(BF16)
+            mine[slot, 2 * d :, :] = dot(dyt[...], prod[...]).T.astype(BF16)
+            tick(number * period + j, 1)
             return 0
 
         lax.fori_loop(0, blocks, block, 0)
 
-        if need:
-
-            def leave(t, _):
-                span = rows(t * TILE, TILE)
-                da = (dag[span, :].astype(BF16).astype(F32) + dau[span, :].astype(BF16).astype(F32)).astype(BF16).astype(F32)
-                wide = h[l, span, :].astype(F32)
-                scale = lax.rsqrt(jnp.mean(wide * wide, -1, keepdims=True) + 1e-6)
-                by_scale = jnp.sum(da * wide, -1, keepdims=True)
-                by_wide = da * scale - wide * (by_scale * scale * scale * scale * (1.0 / d))
-                dy[span, :] = (dy[span, :].astype(F32) + by_wide.astype(BF16).astype(F32)).astype(BF16)
-                return 0
-
-            lax.fori_loop(0, tiles, leave, 0)
+        def between(v, _):
+            for odd in range(2):
+                leave(l, 2 * v + odd)
+                enter(l - 1, 2 * v + odd)
+                tick(number * period + blocks + v, odd)
+            return 0
+
+        if l > 0:
+            lax.fori_loop(0, tiles // 2, between, 0)
 
     def drain(b, _):
         tick(b, 0)
         tick(b, 1)
         return 0
 
-    lax.fori_loop(chunks, chunks + (GATHER_AT[-1] + 1) // 2, drain, 0)
+    done = (layers - 1) * period + blocks
+    lax.fori_loop(done, done + (GATHER_AT[-1] + 1) // 2, drain, 0)
     for c in range(chunks):
         out_copy(c).wait()
 
@@ -325,10 +329,8 @@
             pltpu.VMEM((d, tokens), BF16),
             pltpu.VMEM((d, tokens), BF16),
             pltpu.VMEM((tokens, BLOCK), BF16),
-            pltpu.VMEM((tokens, BLOCK), BF16),
-            pltpu.VMEM((tokens, BLOCK), BF16),
-            pltpu.VMEM((tokens, d), F32),
-            pltpu.VMEM((tokens, d), F32),
+            pltpu.VMEM((blocks, tokens, BLOCK), BF16),
+            pltpu.VMEM((blocks, tokens, BLOCK), BF16),
             pltpu.VMEM(((layers - 1) * blocks, chunk_rows, d), BF16),
             pltpu.VMEM((2, chunk_rows, d), BF16),
             pltpu.VMEM((2, 2, 2, klass, d // 2), BF16),

time: 233 us -> 225 us (0.966)
  Pallas kernels: 232 us -> 224 us
    pallas_call x1, Pallas kernels: 188 us -> 181 us  [summed_gradients(): pl.pallas_call(functools.partial(train_kernel, n), out_shape=jax.ShapeDty...]
where the time goes in v3:
time: 225 us
  Pallas kernels  224 us (100%)
    pallas_call x1, Pallas kernels, summed_gradients(): pl.pallas_call(functools.partial(train_kernel, n), out_shape=jax.ShapeDty...  181 us
    pallas_call x1, Pallas kernels, adamw(): pl.pallas_call(adamw_kernel, grid=(layers * blocks, cut), out_shape=[jax....  43.6 us

profile of v3, /device:TPU:96, one launch (start us, length us, event | category | flops | bytes accessed | tf_op | source)
XLA Modules:
  0.0 225.1 jit_solution(8051854164738586812)
XLA Ops:
  0.6 180.7 %train.1 = bf16[8,1536,512]{2,1,0:T(8,128)(2,1)} custom-call(bf16[1,2048,512]{2,1,0:T(8,128)(2,1)} %x_hbm.1, bf16[1,2048,512]{2,1,0:T(8,128)(2,1)} %dy_hbm.1, bf16[2,512,2048]{2,1,0:T(8,128)(2,1)} %refs_0_.1, bf16[2,512,2048]{2,1,0:T(8,128)(2,1)} %refs_1_.1, bf16[2,2048,512]{2,1,0:T(8,128)(2,1)} %refs_2_.1), custom_call_target="tpu_custom_call" | custom-call | tf_op jit(solution)/shard_map/train/pallas_call | solution.py:320
  181.4 43.6 %adamw.1 = (bf16[2,512,2048]{2,1,0:T(8,128)(2,1)}, bf16[2,512,2048]{2,1,0:T(8,128)(2,1)}, bf16[2,2048,512]{2,1,0:T(8,128)(2,1)}, f32[2,512,2048]{2,1,0:T(8,128)}...) custom-call(bf16[8,3,512,512]{3,2,1,0:T(8,128)(2,1)} %bitcast.1, ...), custom_call_target="tpu_custom_call" | custom-call | tf_op jit(solution)/shard_map/adamw/pallas_call | solution.py:379

commit v4 on v3

--- a/solution.py
+++ b/solution.py
@@ -93,7 +93,8 @@
         for j in range(blocks):
             for copy in w_copies(l, j):
                 copy.start()
-    dy_copy.start()
+        if l == 0:
+            dy_copy.start()
 
     barrier = pltpu.get_barrier_semaphore()
     for other in (*ids["x"], *ids["y"]):
@@ -198,6 +199,14 @@
                 event = functools.partial(ag_event if gather else rs_event, number * blocks + j, e)
                 pl.when((number >= 0) & (number < layers) & (j < blocks))(event)
 
+    def enter(l, t):
+        span = rows(t * TILE, TILE)
+        across = pl.ds(pl.multiple_of(t * TILE, 128), TILE)
+        av = normed(h[l, span, :].astype(F32)).astype(BF16)
+        a[span, :] = av
+        at[:, across] = av.T
+        dyt[:, across] = dy[span, :].T
+
     x_copy.wait()
     for l in range(layers - 1):
         def arrived(l, j):
@@ -216,6 +225,9 @@
                 term = dot(p, w_read(l, j, 2))
                 acc = term if acc is None else acc + term
             h[l + 1, span, :] = (wide + acc.astype(BF16).astype(F32)).astype(BF16)
+            if l == layers - 2:
+                pl.when(t == 0)(dy_copy.wait)
+                enter(l + 1, t)
             return 0
 
         lax.fori_loop(0, tiles, forward, 0)
@@ -223,15 +235,6 @@
     for j in range(blocks):
         for copy in w_copies(layers - 1, j):
             copy.wait()
-    dy_copy.wait()
-
-    def enter(l, t):
-        span = rows(t * TILE, TILE)
-        across = pl.ds(pl.multiple_of(t * TILE, 128), TILE)
-        av = normed(h[l, span, :].astype(F32)).astype(BF16)
-        a[span, :] = av
-        at[:, across] = av.T
-        dyt[:, across] = dy[span, :].T
 
     def leave(l, t):
         span = rows(t * TILE, TILE)
@@ -250,11 +253,6 @@
         by_wide = da * scale - wide * (by_scale * scale * scale * scale * (1.0 / d))
         dy[span, :] = (dy[span, :].astype(F32) + by_wide.astype(BF16).astype(F32)).astype(BF16)
 
-    def first(t, _):
-        enter(layers - 1, t)
-        return 0
-
-    lax.fori_loop(0, tiles, first, 0)
     for number, l in enumerate(reversed(range(layers))):
 
         def block(j, _):

time: 225 us -> 225 us (level)
  no operation moved by 1% of the time
where the time goes in v4:
time: 225 us
  Pallas kernels  224 us (100%)
    pallas_call x1, Pallas kernels, summed_gradients(): pl.pallas_call(functools.partial(train_kernel, n), out_shape=jax.ShapeDty...  181 us
    pallas_call x1, Pallas kernels, adamw(): pl.pallas_call(adamw_kernel, grid=(layers * blocks, cut), out_shape=[jax....  43.6 us

profile of v4, /device:TPU:96, one launch (start us, length us, event | category | flops | bytes accessed | tf_op | source)
XLA Modules:
  0.0 225.1 jit_solution(2237771250392554502)
XLA Ops:
  0.6 180.7 %train.1 = bf16[8,1536,512]{2,1,0:T(8,128)(2,1)} custom-call(bf16[1,2048,512]{2,1,0:T(8,128)(2,1)} %x_hbm.1, bf16[1,2048,512]{2,1,0:T(8,128)(2,1)} %dy_hbm.1, bf16[2,512,2048]{2,1,0:T(8,128)(2,1)} %refs_0_.1, bf16[2,512,2048]{2,1,0:T(8,128)(2,1)} %refs_1_.1, bf16[2,2048,512]{2,1,0:T(8,128)(2,1)} %refs_2_.1), custom_call_target="tpu_custom_call" | custom-call | tf_op jit(solution)/shard_map/train/pallas_call | solution.py:318
  181.4 43.6 %adamw.1 = (bf16[2,512,2048]{2,1,0:T(8,128)(2,1)}, bf16[2,512,2048]{2,1,0:T(8,128)(2,1)}, bf16[2,2048,512]{2,1,0:T(8,128)(2,1)}, f32[2,512,2048]{2,1,0:T(8,128)}...) custom-call(bf16[8,3,512,512]{3,2,1,0:T(8,128)(2,1)} %bitcast.1, ...), custom_call_target="tpu_custom_call" | custom-call | tf_op jit(solution)/shard_map/adamw/pallas_call | solution.py:377
